TPU v7x, 32 devices: a whole 2x2x4 slice. The times are simulated.
32 devices in a mesh: gx: 4 (over x, core), gy: 8 (over z, y).
Axes of the slice: x: 2, y: 2, z: 4, core: 2. Of those that a mesh axis runs over, the one named last changes fastest.
Arguments:
- state: float32 [256, 2, 128, 128], P(('gx', 'gy')), may hold values from -6 to 6
- hamiltonian: float32 [2, 128, 128], replicated, may hold values from -0.5 to 0.5
- couplings: float32 [16, 128, 128], replicated, may hold values from -0.125 to 0.125
- bath_coef: float32 [2, 16], replicated, may hold values from 0.2 to 1
- bath_rate: float32 [16], replicated, may hold values from 0.02 to 0.2
- occupation: int32 [256, 16], P(('gx', 'gy')), may hold values from 0 to 5
- send_list: int32 [32, 32, 1], P(('gx', 'gy')), may hold values from -1 to 7
- up_index: int32 [256, 16], P(('gx', 'gy')), may hold values from -1 to 39
- down_index: int32 [256, 16], P(('gx', 'gy')), may hold values from -1 to 39
- step: float32 [1], replicated, may hold values from 0.5 to 1.5
Outputs:
- derivative: float32 [256, 2, 128, 128], P(('gx', 'gy'))
- advanced: float32 [256, 2, 128, 128], P(('gx', 'gy'))
All inputs are finite; a program needn't handle non-finite values.
Results may differ from a plain program's by a relative error of at most 0.0003.
Values sent between devices are 32-bit elements; how exact they have to be, the bound alone decides.
A program may use at most 256 MiB of HBM per device.

v0:
```python
import functools

import jax
import jax.numpy as jnp
from jax import lax
from jax.experimental import pallas as pl
from jax.experimental.pallas import tpu as pltpu
from jax.sharding import PartitionSpec as P

AXES = ("gx", "gy")
MESH = pl.DeviceIdType.MESH


def split(value):
    high = value.astype(jnp.bfloat16)
    low = (value - high.astype(jnp.float32)).astype(jnp.bfloat16)
    return high, low


def put(n_size, mode, rows, xr, xi, yr, yi, x_hi, x_lo, y_all):
    start, size = rows
    at = pl.ds(mode * n_size + start, size)
    cols = pl.ds(mode * n_size, n_size)
    for part, value in enumerate((xr, xi)):
        high, low = split(value)
        lanes = pl.ds(part * n_size, n_size)
        x_hi[at, lanes] = high
        x_lo[at, lanes] = low
    for part, value in enumerate((yr, yi)):
        high, low = split(value)
        y_all[pl.ds(part * n_size + start, size), cols] = high
        y_all[pl.ds((2 + part) * n_size + start, size), cols] = low


def build_modes(n, offset, source, up, down, occ, coef, x_hi, x_lo, y_all):
    modes = up.shape[1]
    entries, _, size, n_size = source[0].shape
    chunk = min(32, size)
    for k in range(modes):
        iu = up[n, k] - offset
        iw = down[n, k] - offset
        has_u = jnp.logical_and(iu >= 0, iu < entries)
        has_w = jnp.logical_and(iw >= 0, iw < entries)
        mu = jnp.where(has_u, 1.0, 0.0).astype(jnp.float32)
        mw = jnp.where(has_w, occ[n, k], 0).astype(jnp.float32)
        iu = jnp.clip(iu, 0, entries - 1)
        iw = jnp.clip(iw, 0, entries - 1)
        a = mw * coef[0, k]
        b = mw * coef[1, k]
        for start in range(0, n_size, chunk):
            part, rows = source[start // size], pl.ds(start % size, chunk)
            ur, ui = part[iu, 0, rows, :], part[iu, 1, rows, :]
            wr, wi = part[iw, 0, rows, :], part[iw, 1, rows, :]
            p = ur * mu + a * wr
            q = b * wi
            r = ui * mu + a * wi
            s = b * wr
            put(n_size, k, (start, chunk), p - q, r + s, p + q, r - s, x_hi, x_lo, y_all)


def products(n_size, x_hi, x_lo, y_all, q_left, q_right):
    dot = functools.partial(jnp.dot, preferred_element_type=jnp.float32)
    both = dot(q_left[...], x_hi[...])
    left = both[:n_size] + both[n_size:] + dot(q_left[:n_size, :], x_lo[...])
    right = dot(y_all[...], q_right[...])
    two = 2 * n_size
    right = right[:two, :n_size] + right[:two, n_size:] + right[two:, :n_size]
    return left[:, :n_size] - right[:n_size], left[:, n_size:] - right[n_size:]


def fill_matrices(mode, matrix, q_left, q_right):
    n_size = matrix.shape[0]
    high, low = split(matrix)
    at = pl.ds(mode * n_size, n_size)
    q_left[pl.ds(0, n_size), at] = high
    q_left[pl.ds(n_size, n_size), at] = low
    q_right[at, pl.ds(0, n_size)] = high
    q_right[at, pl.ds(n_size, n_size)] = low


def kernel(
    gx, gy, length, halves,
    up, down, occ, coef, rate, step, lists, state, couplings, hamiltonian,
    derivative, advanced,
    below, above, stage, arrived, list_v, list_s, x_hi, x_lo, y_all, x_hi_2, x_lo_2, y_all_2, q_left, q_right, squares, gathered,
    load_sem, up_sem, down_sem, below_sem, above_sem, list_send, list_recv, list_load, plane_send, plane_recv, sum_send, sum_recv,
):
    rows, modes = up.shape
    n_size = state.shape[2]
    count = gx * gy
    side = gy // length
    columns = gx * side
    slots = arrived.shape[0] // count
    x, y = lax.axis_index("gx"), lax.axis_index("gy")
    me = x * gy + y
    z, yy = y // side, lax.rem(y, side)
    column = x * side + yy
    size = n_size // halves

    def place(at, level):
        return at // side, level * side + lax.rem(at, side)

    def strip(half):
        return pl.ds(half * size, size)

    barrier = pltpu.get_barrier_semaphore()

    def load(half):
        return pltpu.make_async_copy(state.at[:, :, strip(half)], below[0][half], load_sem.at[half])

    for half in range(halves):
        load(half).start()

    @pl.loop(1, count)
    def _(hop):
        other = lax.rem(me + hop, count)
        pl.semaphore_signal(barrier, inc=1, device_id=(other // gy, lax.rem(other, gy)), device_id_type=MESH)

    pl.semaphore_wait(barrier, count - 1)

    def relay(hop, half, way):
        held = below if way > 0 else above
        return pltpu.make_async_remote_copy(
            src_ref=(held if hop else below)[hop][half],
            dst_ref=held[hop + 1][half],
            send_sem=(up_sem if way > 0 else down_sem).at[hop, half],
            recv_sem=(below_sem if way > 0 else above_sem).at[hop + 1, half],
            device_id=place(column, z + way),
            device_id_type=MESH,
        )

    def hand(level, hop, half, slot):
        source = place(column, level)
        return pltpu.make_async_remote_copy(
            src_ref=stage.at[level, hop, slot, :, strip(half)],
            dst_ref=arrived.at[(source[0] * gy + source[1]) * slots + slot, :, strip(half)],
            send_sem=plane_send.at[level, hop, slot, half],
            recv_sem=plane_recv.at[level, hop, slot, half],
            device_id=place(lax.rem(column + hop, columns), z),
            device_id_type=MESH,
        )

    def send_lists(hop):
        return pltpu.make_async_remote_copy(
            src_ref=lists,
            dst_ref=list_v.at[z],
            send_sem=list_send.at[hop],
            recv_sem=list_recv.at[hop],
            device_id=place(column, lax.rem(z + hop, length)),
            device_id_type=MESH,
        )

    for hop in range(1, length):
        send_lists(hop).start()
    for half in range(halves):
        load(half).wait()

        @pl.when(z + 1 < length)
        def _():
            relay(0, half, 1).start()

        @pl.when(z > 0)
        def _():
            relay(0, half, -1).start()

    own = pltpu.make_async_copy(lists, list_s.at[z], list_load.at[0])
    own.start()
    own.wait()

    def chosen(held, level, at, slot):
        target = place(at, z)
        entry = (target[0] * gy + target[1]) * slots + slot
        pick = list_s[level, entry // 128, lax.rem(entry, 128)]
        keep = jnp.where(pick < 0, 0.0, 1.0).astype(jnp.float32)
        pick = jnp.clip(pick, 0, rows - 1)
        return held[pick] * keep

    def distribute(held, level, half):
        source = place(column, level)
        first = (source[0] * gy + source[1]) * slots
        for slot in range(slots):

            @pl.loop(1, columns)
            def _(hop):
                stage[level, hop, slot, :, strip(half), :] = chosen(held, level, lax.rem(column + hop, columns), slot)
                hand(level, hop, half, slot).start()

            arrived[first + slot, :, strip(half), :] = chosen(held, level, column, slot)

    for half in range(halves):
        distribute(below[0][half], z, half)

    def arrive(hop, half):
        low, high = z - hop, z + hop

        @pl.when(low >= 0)
        def _():
            relay(hop - 1, half, 1).wait_recv()
            if hop + 1 < length:

                @pl.when(z + 1 < length)
                def _():
                    relay(hop, half, 1).start()

        @pl.when(high < length)
        def _():
            relay(hop - 1, half, -1).wait_recv()
            if hop + 1 < length:

                @pl.when(z > 0)
                def _():
                    relay(hop, half, -1).start()

        @pl.when(low >= 0)
        def _():
            distribute(below[hop][half], low, half)

        @pl.when(high < length)
        def _():
            distribute(above[hop][half], high, half)

    for k in range(modes):
        fill_matrices(k, couplings[k], q_left, q_right)
    for k in range(2):
        fill_matrices(modes + k, hamiltonian[k], q_left, q_right)
    here = below[0]

    def local_part(n):
        build_modes(n, 0, here, up, down, occ, coef, x_hi, x_lo, y_all)
        chunk = min(32, size)
        for start in range(0, n_size, chunk):
            part, at = here[start // size], pl.ds(start % size, chunk)
            re, im = part[n, 0, at, :], part[n, 1, at, :]
            put(n_size, modes, (start, chunk), re, im, re, im, x_hi, x_lo, y_all)
            put(n_size, modes + 1, (start, chunk), -im, re, -im, re, x_hi, x_lo, y_all)
        re, im = products(n_size, x_hi, x_lo, y_all, q_left, q_right)
        damping = jnp.float32(0)
        for k in range(modes):
            damping += occ[n, k].astype(jnp.float32) * rate[k]
        for half in range(halves):
            at = slice(half * size, (half + 1) * size)
            derivative[n, 0, strip(half)] = im[at] - damping * here[half][n, 0]
            derivative[n, 1, strip(half)] = -re[at] - damping * here[half][n, 1]

    for hop in range(1, length):
        send_lists(hop).wait()
    for hop in range(1, length):
        level = lax.rem(z + hop, length)
        copy = pltpu.make_async_copy(list_v.at[level], list_s.at[level], list_load.at[hop])
        copy.start()
        copy.wait()

    turns = 2 if rows % 2 == 0 and halves % 2 == 0 else 1
    share, strips = rows // turns, halves // turns
    for turn in range(turns):

        @pl.loop(0, share)
        def _(n):
            local_part(turn * share + n)

        for half in range(turn * strips, (turn + 1) * strips):
            arrive(1, half)

    for hop in range(2, length):
        for half in range(halves):
            arrive(hop, half)

    for level in range(length):

        @pl.loop(1, columns)
        def _(hop):
            for slot in range(slots):
                for half in range(halves):
                    hand(level, hop, half, slot).wait_recv()

    squares[...] = jnp.zeros_like(squares)
    depth = modes * n_size

    first = (x_hi.at[:depth], x_lo.at[:depth], y_all.at[:, :depth])
    second = (x_hi_2, x_lo_2, y_all_2)

    def build(n, operands):
        build_modes(n, rows, [arrived], up, down, occ, coef, *operands)

    def finish(n, operands):
        re, im = products(n_size, *operands, q_left.at[:, :depth], q_right.at[:depth])
        re, im = derivative[n, 0] + im, derivative[n, 1] - re
        derivative[n, 0] = re
        derivative[n, 1] = im
        total = re * re + im * im
        squares[...] += jnp.sum(total.reshape(n_size // 8, 8, n_size), axis=0)

    build(0, first)

    @pl.loop(0, rows // 2)
    def _(pair):
        n = pair * 2
        build(n + 1, second)
        finish(n, first)
        build(jnp.minimum(n + 2, rows - 1), first)
        finish(n + 1, second)

    if rows % 2:
        finish(rows - 1, first)

    def copy_to(hop):
        other = lax.rem(me + hop, count)
        return pltpu.make_async_remote_copy(
            src_ref=squares,
            dst_ref=gathered.at[hop],
            send_sem=sum_send.at[hop],
            recv_sem=sum_recv.at[hop],
            device_id=(other // gy, lax.rem(other, gy)),
            device_id_type=MESH,
        )

    @pl.loop(1, count)
    def _(hop):
        copy_to(hop).start()

    gathered[0] = squares[...]
    for level in range(length):

        @pl.loop(1, columns)
        def _(hop):
            for slot in range(slots):
                for half in range(halves):
                    hand(level, hop, half, slot).wait_send()

    for hop in range(length - 1):
        for half in range(halves):

            @pl.when(jnp.logical_and(z >= hop, z + 1 < length))
            def _():
                relay(hop, half, 1).wait_send()

            @pl.when(jnp.logical_and(z + hop < length, z > 0))
            def _():
                relay(hop, half, -1).wait_send()

    @pl.loop(1, count)
    def _(hop):
        copy_to(hop).wait()

    total = jnp.sum(jnp.sum(gathered[...], axis=0), axis=(0, 1), keepdims=True)
    scale = step[0] / jnp.sqrt(total / (rows * count * 2 * n_size * n_size) + 1e-06)

    @pl.loop(0, rows)
    def _(n):
        for part in range(2):
            for half in range(halves):
                value = here[half][n, part] + scale * derivative[n, part, strip(half)]
                advanced[n, part, strip(half)] = value


def smem():
    return pl.BlockSpec(memory_space=pltpu.SMEM)


def vmem():
    return pl.BlockSpec(memory_space=pltpu.VMEM)


def line_length(gx, gy):
    side = max(gx // 2, 1)
    return gy // side if gy % side == 0 else gy


def make_body(gx, gy):
    count = gx * gy
    length = line_length(gx, gy)
    columns = count // length

    def body(state, hamiltonian, couplings, bath_coef, bath_rate, occupation, send_list, up_index, down_index, step):
        rows, parts, n_size, _ = state.shape
        modes = couplings.shape[0]
        slots = send_list.shape[2]
        halves = 4 if n_size % 32 == 0 else 1
        chosen = send_list.reshape(-1)
        lanes = 128
        deep = -(-chosen.shape[0] // (8 * lanes)) * 8
        lists = jnp.pad(chosen, (0, deep * lanes - chosen.shape[0])).reshape(deep, lanes)
        depth = (modes + 2) * n_size
        tile = state.shape[1:]
        piece = pltpu.VMEM((rows, parts, n_size // halves, n_size), state.dtype)
        strips = tuple((piece,) * halves for _ in range(length))
        f32, bf16, i32 = jnp.float32, jnp.bfloat16, jnp.int32
        dma = pltpu.SemaphoreType.DMA
        return pl.pallas_call(
            functools.partial(kernel, gx, gy, length, halves),
            out_shape=(jax.ShapeDtypeStruct(state.shape, f32), jax.ShapeDtypeStruct(state.shape, f32)),
            in_specs=[smem()] * 6 + [vmem(), pl.BlockSpec(memory_space=pl.ANY), vmem(), vmem()],
            out_specs=(vmem(), vmem()),
            scratch_shapes=[
                strips,
                ((pltpu.VMEM((1, 1, 8, n_size), f32),) * halves,) + strips[1:],
                pltpu.VMEM((length, columns, slots) + tile, f32),
                pltpu.VMEM((count * slots,) + tile, f32),
                pltpu.VMEM((length, deep, lanes), i32),
                pltpu.SMEM((length, deep, lanes), i32),
                pltpu.VMEM((depth, 2 * n_size), bf16),
                pltpu.VMEM((depth, 2 * n_size), bf16),
                pltpu.VMEM((4 * n_size, depth), bf16),
                pltpu.VMEM((modes * n_size, 2 * n_size), bf16),
                pltpu.VMEM((modes * n_size, 2 * n_size), bf16),
                pltpu.VMEM((4 * n_size, modes * n_size), bf16),
                pltpu.VMEM((2 * n_size, depth), bf16),
                pltpu.VMEM((depth, 2 * n_size), bf16),
                pltpu.VMEM((8, n_size), f32),
                pltpu.VMEM((count, 8, n_size), f32),
                dma((halves,)),
                dma((length, halves)),
                dma((length, halves)),
                dma((length, halves)),
                dma((length, halves)),
                dma((length,)),
                dma((length,)),
                dma((length,)),
                dma((length, columns, slots, halves)),
                dma((length, columns, slots, halves)),
                dma((count,)),
                dma((count,)),
            ],
            compiler_params=pltpu.CompilerParams(collective_id=0, has_side_effects=True, vmem_limit_bytes=60 << 20),
            name="step",
        )(up_index, down_index, occupation, bath_coef, bath_rate, step, lists, state, couplings, hamiltonian)

    return body


def solution(mesh):
    placed = (
        P(AXES, None, None, None),
        P(),
        P(),
        P(),
        P(),
        P(AXES, None),
        P(AXES, None, None),
        P(AXES, None),
        P(AXES, None),
        P(),
    )
    return jax.shard_map(
        make_body(mesh.shape["gx"], mesh.shape["gy"]),
        mesh=mesh,
        in_specs=placed,
        out_specs=(P(AXES, None, None, None), P(AXES, None, None, None)),
        check_vma=False,
    )
```

profile of v0, /device:TPU:0, one launch (start us, length us, event | category | flops | bytes accessed | tf_op | source)
XLA Modules:
  0.0 113.9 jit_solution(4519168603550362069)
XLA Ops:
  1.3 0.0 copy-start.1
  1.3 0.6 copy-done.1
  1.9 0.6 pad_bitcast_fusion.lists
  2.5 108.0 %step.2 = (f32[8,2,128,128]{3,2,1,0:T(8,128)}, f32[8,2,128,128]{3,2,1,0:T(8,128)}) custom-call(s32[8,16]{1,0:T(8,128)} %up.1, s32[8,16]{1,0:T(8,128)} %down.1, s32[8,16]{1,0:T(8,128)} %occ.1, f32[2,16]{1,0:T(2,128)} %coef.1, f32[16]{0:T(128)} %rate.1, f32[1]{0:T(128)S(6)} %copy.14.step, s32[8,128]{1,0:T(8,128)} %pad_bitcast_fusion.lists, ...), custom_call_target="tpu_custom_call" | custom-call | tf_op jit(solution)/shard_map/step/pallas_call | solution.py:389
  110.5 0.0 copy-start
  110.5 2.4 %copy.15 = f32[8,2,128,128]{3,2,1,0:T(8,128)} copy(f32[8,2,128,128]{3,2,1,0:T(8,128)} %get-tuple-element.4) | data formatting | bytes 2097152
  112.9 0.0 copy-done
  112.9 1.0 copy.16
Async XLA Ops:
  1.3 0.7 copy-start.1
  110.5 2.4 %copy-start = (f32[8,2,128,128]{3,2,1,0:T(8,128)S(1)}, f32[8,2,128,128]{3,2,1,0:T(8,128)}, u32[]{:S(2)}) copy-start(f32[8,2,128,128]{3,2,1,0:T(8,128)} %get-tuple-element.5) | copy-start | bytes 3145732
where the time goes:
time: 114 us
  Pallas kernels  108 us (95%)
  local copies, waits for them, and re-layouts  4.6 us (4%)
  between operations  1.3 us (1%)
    pallas_call x1, Pallas kernels, body(): pl.pallas_call(functools.partial(kernel, gx, gy, length, halves), out_sha...  108 us
    unnamed x6, local copies, waits for them, and re-layouts  4.01 us

commit v1 on v0

v1 whole, which is shorter than its diff:
```python
import functools

import jax
import jax.numpy as jnp
from jax import lax
from jax.experimental import pallas as pl
from jax.experimental.pallas import tpu as pltpu
from jax.sharding import PartitionSpec as P

AXES = ("gx", "gy")
MESH = pl.DeviceIdType.MESH
COMPUTE = True


def split(value):
    high = value.astype(jnp.bfloat16)
    low = (value - high.astype(jnp.float32)).astype(jnp.bfloat16)
    return high, low


def kernel(
    gx, gy, length, strips,
    up, down, occ, coef, rate, step, lists, state, couplings, hamiltonian,
    derivative, advanced,
    own, below, above, arrived, stage, list_v, list_s, from_u, from_w, scale_a, scale_b,
    q_full, q_turned, q_left, q_right, h_full, h_left, h_right, h_x_hi, h_x_lo, h_y,
    x_hi, x_lo, x_hi_2, x_lo_2, y_hi, y_lo, der, adv, squares, gathered,
    load_sem, copy_sem, q_sem, up_sem, down_sem, below_sem, above_sem, list_send, list_recv, list_load, plane_send, plane_recv,
    sum_send, sum_recv, out_sem,
):
    rows, modes = up.shape
    n_size = state.shape[2]
    count = gx * gy
    side = gy // length
    columns = gx * side
    slots = lists.shape[1]
    size = n_size // strips
    x, y = lax.axis_index("gx"), lax.axis_index("gy")
    me = x * gy + y
    z, yy = y // side, lax.rem(y, side)
    column = x * side + yy
    dot = functools.partial(jnp.dot, preferred_element_type=jnp.float32)

    def place(at, level):
        return at // side, level * side + lax.rem(at, side)

    def strip(h):
        return pl.ds(h * size, size)

    barrier = pltpu.get_barrier_semaphore()

    def load(h):
        return pltpu.make_async_copy(state.at[:, :, strip(h)], own[h], load_sem.at[h])

    def load_again(h):
        return pltpu.make_async_copy(state.at[:, :, strip(h)], arrived[h].at[pl.ds(0, rows)], copy_sem.at[h])

    for h in range(strips):
        load(h).start()
    load_list = pltpu.make_async_copy(lists.at[0], list_s.at[z], list_load.at[0])
    load_list.start()

    @pl.loop(1, count)
    def _(hop):
        other = lax.rem(me + hop, count)
        pl.semaphore_signal(barrier, inc=1, device_id=(other // gy, lax.rem(other, gy)), device_id_type=MESH)

    for h in range(strips):
        load_again(h).start()
    load_q = pltpu.make_async_copy(couplings, q_full, q_sem.at[0])
    load_h = pltpu.make_async_copy(hamiltonian, h_full, q_sem.at[1])
    load_q.start()
    load_h.start()
    pl.semaphore_wait(barrier, count - 1)

    def relay(hop, h, way):
        held = below if way > 0 else above
        return pltpu.make_async_remote_copy(
            src_ref=held[hop - 1][h] if hop else own[h],
            dst_ref=held[hop][h],
            send_sem=(up_sem if way > 0 else down_sem).at[hop, h],
            recv_sem=(below_sem if way > 0 else above_sem).at[hop, h],
            device_id=place(column, z + way),
            device_id_type=MESH,
        )

    def send_lists(hop):
        return pltpu.make_async_remote_copy(
            src_ref=lists.at[0],
            dst_ref=list_v.at[z],
            send_sem=list_send.at[hop],
            recv_sem=list_recv.at[hop],
            device_id=place(column, lax.rem(z + hop, length)),
            device_id_type=MESH,
        )

    for hop in range(1, length):
        send_lists(hop).start()
    for h in range(strips):
        load(h).wait()

        @pl.when(z + 1 < length)
        def _():
            relay(0, h, 1).start()

        @pl.when(z > 0)
        def _():
            relay(0, h, -1).start()

    load_list.wait()

    def hand(level, h, hop, slot):
        return pltpu.make_async_remote_copy(
            src_ref=stage.at[level, h, hop * slots + slot],
            dst_ref=arrived[h].at[rows + (level * columns + hop) * slots + slot],
            send_sem=plane_send.at[level, h],
            recv_sem=plane_recv.at[level, h],
            device_id=place(lax.rem(column + hop, columns), z),
            device_id_type=MESH,
        )

    def all_hands(level, h):
        part = pl.ds(slots, (columns - 1) * slots)
        return pltpu.make_async_remote_copy(
            src_ref=stage.at[level, h, part],
            dst_ref=arrived[h].at[pl.ds(rows + (level * columns + 1) * slots, (columns - 1) * slots)],
            send_sem=plane_send.at[level, h],
            recv_sem=plane_recv.at[level, h],
            device_id=place(lax.rem(column + 1, columns), z),
            device_id_type=MESH,
        )

    def chosen(held, level, at, slot):
        target = place(at, z)
        pick = list_s[level, slot, target[0] * gy + target[1]]
        keep = jnp.where(pick < 0, 0.0, 1.0).astype(jnp.float32)
        pick = jnp.clip(pick, 0, rows - 1)
        return held[pick] * keep

    def distribute(held, level, h):
        for slot in range(slots):

            @pl.loop(1, columns)
            def _(hop):
                stage[level, h, hop * slots + slot] = chosen(held, level, lax.rem(column + hop, columns), slot)
                hand(level, h, hop, slot).start()

            arrived[h][rows + level * columns * slots + slot] = chosen(held, level, column, slot)

    for h in range(strips):
        distribute(own[h], z, h)

    def arrive(hop, h):
        low, high = z - hop, z + hop

        @pl.when(low >= 0)
        def _():
            relay(hop - 1, h, 1).wait_recv()
            if hop + 1 < length:

                @pl.when(z + 1 < length)
                def _():
                    relay(hop, h, 1).start()

        @pl.when(high < length)
        def _():
            relay(hop - 1, h, -1).wait_recv()
            if hop + 1 < length:

                @pl.when(z > 0)
                def _():
                    relay(hop, h, -1).start()

        @pl.when(low >= 0)
        def _():
            distribute(below[hop - 1][h], low, h)

        @pl.when(high < length)
        def _():
            distribute(above[hop - 1][h], high, h)

    for hop in range(1, length):
        send_lists(hop).wait()
    for hop in range(1, length):
        level = lax.rem(z + hop, length)
        copy = pltpu.make_async_copy(list_v.at[level], list_s.at[level], list_load.at[hop])
        copy.start()
        copy.wait()

    load_q.wait()
    load_h.wait()
    for k in range(modes):
        high, low = split(q_full[k])
        at = pl.ds(k * n_size, n_size)
        q_right[at, pl.ds(0, n_size)] = high
        q_right[at, pl.ds(n_size, n_size)] = low
        q_turned[k] = q_full[k].T
    for k in range(2):
        high, low = split(h_full[k])
        at = pl.ds(k * n_size, n_size)
        h_right[at, pl.ds(0, n_size)] = high
        h_right[at, pl.ds(n_size, n_size)] = low
        h_left[pl.ds(0, n_size), at] = high
        h_left[pl.ds(n_size, n_size), at] = low

    for h in range(strips):
        arrive(1, h)

    for h in range(strips):
        turned = q_turned[:, h * size:(h + 1) * size, :].reshape(modes * size, n_size).T
        high, low = split(turned)
        q_left[h, pl.ds(0, n_size), :] = high
        q_left[h, pl.ds(n_size, n_size), :] = low

    empty = rows + count * slots

    def position(index):
        source = (index - rows) // slots
        slot = lax.rem(index - rows, slots) if slots > 1 else 0
        sx, sy = source // gy, lax.rem(source, gy)
        hop = lax.rem(column + columns - (sx * side + lax.rem(sy, side)), columns)
        far = rows + ((sy // side) * columns + hop) * slots + slot
        return jnp.where(index < 0, empty, jnp.where(index < rows, index, far))

    @pl.loop(0, rows)
    def _(n):
        for k in range(modes):
            weight = occ[n, k].astype(jnp.float32)
            from_u[n, k] = position(up[n, k])
            from_w[n, k] = position(down[n, k])
            scale_a[n, k] = weight * coef[0, k]
            scale_b[n, k] = weight * coef[1, k]

    for h in range(strips):
        arrived[h][empty] = jnp.zeros((2, size, n_size), jnp.float32)

    @pl.loop(0, rows)
    def _(n):
        for h in range(strips):
            re, im = own[h][n, 0], own[h][n, 1]
            at, at_2 = strip(h), pl.ds(n_size + h * size, size)
            one, two = pl.ds(0, n_size), pl.ds(n_size, n_size)
            re_hi, re_lo = split(re)
            im_hi, im_lo = split(im)
            h_x_hi[at, one], h_x_hi[at, two] = re_hi, im_hi
            h_x_lo[at, one], h_x_lo[at, two] = re_lo, im_lo
            h_x_hi[at_2, one], h_x_hi[at_2, two] = -im_hi, re_hi
            h_x_lo[at_2, one], h_x_lo[at_2, two] = -im_lo, re_lo
            for part, (first, second) in enumerate(((re_hi, -im_hi), (im_hi, re_hi), (re_lo, -im_lo), (im_lo, re_lo))):
                at_y = pl.ds(part * n_size + h * size, size)
                h_y[at_y, one], h_y[at_y, two] = first, second
        both = dot(h_left[...], h_x_hi[...])
        left = both[:n_size] + both[n_size:] + dot(h_left[:n_size, :], h_x_lo[...])
        right = dot(h_y[...], h_right[...])
        two = 2 * n_size
        right = right[:two, :n_size] + right[:two, n_size:] + right[two:, :n_size]
        damping = jnp.float32(0)
        for k in range(modes):
            damping += occ[n, k].astype(jnp.float32) * rate[k]
        re, im = left[:, :n_size] - right[:n_size], left[:, n_size:] - right[n_size:]
        for h in range(strips):
            at = slice(h * size, (h + 1) * size)
            der[n, 0, strip(h)] = im[at] - damping * own[h][n, 0]
            der[n, 1, strip(h)] = -re[at] - damping * own[h][n, 1]

    for hop in range(2, length - 1):
        for h in range(strips):
            arrive(hop, h)

    def build(h, n, xh, xl):
        source = arrived[h]
        for k in range(modes):
            iu, iw = from_u[n, k], from_w[n, k]
            a, b = scale_a[n, k], scale_b[n, k]
            ur, ui = source[iu, 0], source[iu, 1]
            wr, wi = source[iw, 0], source[iw, 1]
            p, q = ur + a * wr, b * wi
            r, s = ui + a * wi, b * wr
            at = pl.ds(k * size, size)
            for part, value in enumerate((p - q, r + s)):
                lanes = pl.ds(part * n_size, n_size)
                xh[at, lanes], xl[at, lanes] = split(value)
            for part, value in enumerate((p + q, r - s)):
                at_y = pl.ds(pl.multiple_of((n * 2 + part) * size, size), size)
                lanes = pl.ds(k * n_size, n_size)
                y_hi[at_y, lanes], y_lo[at_y, lanes] = split(value)

    def finish(h, n, xh, xl):
        both = dot(q_left[h], xh[...])
        left = both[:n_size] + both[n_size:] + dot(q_left[h, :n_size, :], xl[...])
        der[n, 0] += left[:, n_size:]
        der[n, 1] -= left[:, :n_size]

    def compute(h):
        build(h, 0, x_hi, x_lo)

        @pl.loop(0, rows // 2)
        def _(pair):
            n = pair * 2
            build(h, n + 1, x_hi_2, x_lo_2)
            finish(h, n, x_hi, x_lo)
            build(h, jnp.minimum(n + 2, rows - 2), x_hi, x_lo)
            finish(h, n + 1, x_hi_2, x_lo_2)

        high = dot(y_hi[...], q_right[...])
        right = high[:, :n_size] + high[:, n_size:] + dot(y_lo[...], q_right[:, :n_size])
        for n in range(rows):
            der[n, 0, strip(h)] -= right[(2 * n + 1) * size:(2 * n + 2) * size]
            der[n, 1, strip(h)] += right[2 * n * size:(2 * n + 1) * size]

    def process(h):
        for level in range(length):
            all_hands(level, h).wait_recv()
        if COMPUTE:
            compute(h)

    for h in range(strips):
        load_again(h).wait()

    last = length - 1
    for h in range(strips):
        arrive(last, h)
        if h:
            process(h - 1)
    process(strips - 1)

    squares[...] = jnp.zeros_like(squares)

    @pl.loop(0, rows)
    def _(n):
        re, im = der[n, 0], der[n, 1]
        total = re * re + im * im
        squares[...] += jnp.sum(total.reshape(n_size // 8, 8, n_size), axis=0)

    def copy_to(hop):
        other = lax.rem(me + hop, count)
        return pltpu.make_async_remote_copy(
            src_ref=squares,
            dst_ref=gathered.at[hop],
            send_sem=sum_send.at[hop],
            recv_sem=sum_recv.at[hop],
            device_id=(other // gy, lax.rem(other, gy)),
            device_id_type=MESH,
        )

    @pl.loop(1, count)
    def _(hop):
        copy_to(hop).start()

    out = pltpu.make_async_copy(der, derivative, out_sem.at[0])
    out.start()
    gathered[0] = squares[...]
    for level in range(length):
        for h in range(strips):
            all_hands(level, h).wait_send()

    for hop in range(length - 1):
        for h in range(strips):

            @pl.when(jnp.logical_and(z >= hop, z + 1 < length))
            def _():
                relay(hop, h, 1).wait_send()

            @pl.when(jnp.logical_and(z + hop < length, z > 0))
            def _():
                relay(hop, h, -1).wait_send()

    @pl.loop(1, count)
    def _(hop):
        copy_to(hop).wait()

    total = jnp.sum(jnp.sum(gathered[...], axis=0), axis=(0, 1), keepdims=True)
    scale = step[0] / jnp.sqrt(total / (rows * count * 2 * n_size * n_size) + 1e-06)

    @pl.loop(0, rows)
    def _(n):
        for part in range(2):
            for h in range(strips):
                adv[n, part, strip(h)] = own[h][n, part] + scale * der[n, part, strip(h)]

    out_2 = pltpu.make_async_copy(adv, advanced, out_sem.at[1])
    out_2.start()
    out.wait()
    out_2.wait()


def smem():
    return pl.BlockSpec(memory_space=pltpu.SMEM)


def hbm():
    return pl.BlockSpec(memory_space=pl.ANY)


def line_length(gx, gy):
    side = max(gx // 2, 1)
    return gy // side if gy % side == 0 else gy


def make_body(gx, gy):
    count = gx * gy
    length = line_length(gx, gy)
    columns = count // length

    def body(state, hamiltonian, couplings, bath_coef, bath_rate, occupation, send_list, up_index, down_index, step):
        rows, parts, n_size, _ = state.shape
        modes = couplings.shape[0]
        slots = send_list.shape[2]
        strips = 8 if n_size % 128 == 0 else 1
        size = n_size // strips
        lists = jnp.swapaxes(send_list, 1, 2)
        f32, bf16, i32 = jnp.float32, jnp.bfloat16, jnp.int32
        vmem, sm, dma = pltpu.VMEM, pltpu.SMEM, pltpu.SemaphoreType.DMA
        piece = vmem((rows, parts, size, n_size), f32)
        held = tuple((piece,) * strips for _ in range(length - 1))
        entries = rows + count * slots + 1
        return pl.pallas_call(
            functools.partial(kernel, gx, gy, length, strips),
            out_shape=(jax.ShapeDtypeStruct(state.shape, f32), jax.ShapeDtypeStruct(state.shape, f32)),
            in_specs=[smem()] * 6 + [hbm()] * 4,
            out_specs=(hbm(), hbm()),
            scratch_shapes=[
                (piece,) * strips,
                held,
                held,
                (vmem((entries, parts, size, n_size), f32),) * strips,
                vmem((length, strips, columns * slots, parts, size, n_size), f32),
                vmem((length, slots, count), i32),
                sm((length, slots, count), i32),
                sm((rows, modes), i32),
                sm((rows, modes), i32),
                sm((rows, modes), f32),
                sm((rows, modes), f32),
                vmem(couplings.shape, f32),
                vmem(couplings.shape, f32),
                vmem((strips, 2 * n_size, modes * size), bf16),
                vmem((modes * n_size, 2 * n_size), bf16),
                vmem(hamiltonian.shape, f32),
                vmem((2 * n_size, 2 * n_size), bf16),
                vmem((2 * n_size, 2 * n_size), bf16),
                vmem((2 * n_size, 2 * n_size), bf16),
                vmem((2 * n_size, 2 * n_size), bf16),
                vmem((4 * n_size, 2 * n_size), bf16),
                vmem((modes * size, 2 * n_size), bf16),
                vmem((modes * size, 2 * n_size), bf16),
                vmem((modes * size, 2 * n_size), bf16),
                vmem((modes * size, 2 * n_size), bf16),
                vmem((rows * 2 * size, modes * n_size), bf16),
                vmem((rows * 2 * size, modes * n_size), bf16),
                vmem(state.shape, f32),
                vmem(state.shape, f32),
                vmem((8, n_size), f32),
                vmem((count, 8, n_size), f32),
                dma((strips,)),
                dma((strips,)),
                dma((2,)),
                dma((length, strips)),
                dma((length, strips)),
                dma((length, strips)),
                dma((length, strips)),
                dma((length,)),
                dma((length,)),
                dma((length,)),
                dma((length, strips)),
                dma((length, strips)),
                dma((count,)),
                dma((count,)),
                dma((2,)),
            ],
            compiler_params=pltpu.CompilerParams(collective_id=0, has_side_effects=True, vmem_limit_bytes=60 << 20),
            name="step",
        )(up_index, down_index, occupation, bath_coef, bath_rate, step, lists, state, couplings, hamiltonian)

    return body


def solution(mesh):
    placed = (
        P(AXES, None, None, None),
        P(),
        P(),
        P(),
        P(),
        P(AXES, None),
        P(AXES, None, None),
        P(AXES, None),
        P(AXES, None),
        P(),
    )
    return jax.shard_map(
        make_body(mesh.shape["gx"], mesh.shape["gy"]),
        mesh=mesh,
        in_specs=placed,
        out_specs=(P(AXES, None, None, None), P(AXES, None, None, None)),
        check_vma=False,
    )
```

time: 114 us -> 100 us (0.88)
  Pallas kernels: 108 us -> 95.4 us
  local copies, waits for them, and re-layouts: 4.6 us -> 3.36 us
    pallas_call x1, Pallas kernels: 108 us -> 95.4 us  [body(): pl.pallas_call(functools.partial(kernel, gx, gy, length, strips), out_sha...]
    unnamed x6 -> x4, local copies, waits for them, and re-layouts: 4.01 us -> 3.36 us
where the time goes in v1:
time: 100 us
  Pallas kernels  95.4 us (95%)
  local copies, waits for them, and re-layouts  3.36 us (3%)
  between operations  1.3 us (1%)
    pallas_call x1, Pallas kernels, body(): pl.pallas_call(functools.partial(kernel, gx, gy, length, strips), out_sha...  95.4 us
    unnamed x4, local copies, waits for them, and re-layouts  3.36 us

profile of v1, /device:TPU:0, one launch (start us, length us, event | category | flops | bytes accessed | tf_op | source)
XLA Modules:
  0.0 100.1 jit_solution(13240210092047442141)
XLA Ops:
  1.3 95.4 %step.2 = (f32[8,2,128,128]{3,2,1,0:T(8,128)}, f32[8,2,128,128]{3,2,1,0:T(8,128)}) custom-call(s32[8,16]{1,0:T(8,128)} %up.1, s32[8,16]{1,0:T(8,128)} %down.1, s32[8,16]{1,0:T(8,128)} %occ.1, f32[2,16]{1,0:T(2,128)} %coef.1, f32[16]{0:T(128)} %rate.1, f32[1]{0:T(128)S(6)} %copy.14.step, s32[1,1,32]{2,1,0:T(1,128)} %bitcast.1, f32[8,2,128,128]{3,2,1,0:T(8,128)} %state.1, ...), custom_call_target="tpu_custom_call" | custom-call | tf_op jit(solution)/shard_map/step/pallas_call | solution.py:417
  96.7 0.0 copy-start
  96.7 2.4 %copy.15 = f32[8,2,128,128]{3,2,1,0:T(8,128)} copy(f32[8,2,128,128]{3,2,1,0:T(8,128)} %get-tuple-element.4) | data formatting | bytes 2097152
  99.1 0.0 copy-done
  99.1 1.0 copy.16
Async XLA Ops:
  96.7 2.4 %copy-start = (f32[8,2,128,128]{3,2,1,0:T(8,128)S(1)}, f32[8,2,128,128]{3,2,1,0:T(8,128)}, u32[]{:S(2)}) copy-start(f32[8,2,128,128]{3,2,1,0:T(8,128)} %get-tuple-element.5) | copy-start | bytes 3145732

commit v2 on v1

--- a/solution.py
+++ b/solution.py
@@ -21,10 +21,10 @@
 def kernel(
     gx, gy, length, strips,
     up, down, occ, coef, rate, step, lists, state, couplings, hamiltonian,
-    derivative, advanced,
+    negative, factor,
     own, below, above, arrived, stage, list_v, list_s, from_u, from_w, scale_a, scale_b,
     q_full, q_turned, q_left, q_right, h_full, h_left, h_right, h_x_hi, h_x_lo, h_y,
-    x_hi, x_lo, x_hi_2, x_lo_2, y_hi, y_lo, der, adv, squares, gathered,
+    x_hi, x_lo, x_hi_2, x_lo_2, y_hi, y_lo, der, squares, gathered,
     load_sem, copy_sem, q_sem, up_sem, down_sem, below_sem, above_sem, list_send, list_recv, list_load, plane_send, plane_recv,
     sum_send, sum_recv, out_sem,
 ):
@@ -60,10 +60,12 @@
     load_list = pltpu.make_async_copy(lists.at[0], list_s.at[z], list_load.at[0])
     load_list.start()
 
-    @pl.loop(1, count)
+    for hop in range(1, length):
+        pl.semaphore_signal(barrier, inc=1, device_id=place(column, lax.rem(z + hop, length)), device_id_type=MESH)
+
+    @pl.loop(1, columns)
     def _(hop):
-        other = lax.rem(me + hop, count)
-        pl.semaphore_signal(barrier, inc=1, device_id=(other // gy, lax.rem(other, gy)), device_id_type=MESH)
+        pl.semaphore_signal(barrier, inc=1, device_id=place(lax.rem(column + hop, columns), z), device_id_type=MESH)
 
     for h in range(strips):
         load_again(h).start()
@@ -71,7 +73,7 @@
     load_h = pltpu.make_async_copy(hamiltonian, h_full, q_sem.at[1])
     load_q.start()
     load_h.start()
-    pl.semaphore_wait(barrier, count - 1)
+    pl.semaphore_wait(barrier, length + columns - 2)
 
     def relay(hop, h, way):
         held = below if way > 0 else above
@@ -260,8 +262,8 @@
         re, im = left[:, :n_size] - right[:n_size], left[:, n_size:] - right[n_size:]
         for h in range(strips):
             at = slice(h * size, (h + 1) * size)
-            der[n, 0, strip(h)] = im[at] - damping * own[h][n, 0]
-            der[n, 1, strip(h)] = -re[at] - damping * own[h][n, 1]
+            der[n, 0, strip(h)] = damping * own[h][n, 0] - im[at]
+            der[n, 1, strip(h)] = damping * own[h][n, 1] + re[at]
 
     for hop in range(2, length - 1):
         for h in range(strips):
@@ -288,8 +290,8 @@
     def finish(h, n, xh, xl):
         both = dot(q_left[h], xh[...])
         left = both[:n_size] + both[n_size:] + dot(q_left[h, :n_size, :], xl[...])
-        der[n, 0] += left[:, n_size:]
-        der[n, 1] -= left[:, :n_size]
+        der[n, 0] -= left[:, n_size:]
+        der[n, 1] += left[:, :n_size]
 
     def compute(h):
         build(h, 0, x_hi, x_lo)
@@ -305,8 +307,8 @@
         high = dot(y_hi[...], q_right[...])
         right = high[:, :n_size] + high[:, n_size:] + dot(y_lo[...], q_right[:, :n_size])
         for n in range(rows):
-            der[n, 0, strip(h)] -= right[(2 * n + 1) * size:(2 * n + 2) * size]
-            der[n, 1, strip(h)] += right[2 * n * size:(2 * n + 1) * size]
+            der[n, 0, strip(h)] += right[(2 * n + 1) * size:(2 * n + 2) * size]
+            der[n, 1, strip(h)] -= right[2 * n * size:(2 * n + 1) * size]
 
     def process(h):
         for level in range(length):
@@ -324,13 +326,12 @@
             process(h - 1)
     process(strips - 1)
 
-    squares[...] = jnp.zeros_like(squares)
-
-    @pl.loop(0, rows)
-    def _(n):
+    def square(n, total):
         re, im = der[n, 0], der[n, 1]
-        total = re * re + im * im
-        squares[...] += jnp.sum(total.reshape(n_size // 8, 8, n_size), axis=0)
+        return total + jnp.sum((re * re + im * im).reshape(n_size // 8, 8, n_size), axis=0)
+
+    total = lax.fori_loop(0, rows, square, jnp.zeros((8, n_size), jnp.float32))
+    squares[...] = jnp.sum(total, axis=0, keepdims=True)
 
     def copy_to(hop):
         other = lax.rem(me + hop, count)
@@ -347,7 +348,7 @@
     def _(hop):
         copy_to(hop).start()
 
-    out = pltpu.make_async_copy(der, derivative, out_sem.at[0])
+    out = pltpu.make_async_copy(der, negative, out_sem.at[0])
     out.start()
     gathered[0] = squares[...]
     for level in range(length):
@@ -372,16 +373,8 @@
     total = jnp.sum(jnp.sum(gathered[...], axis=0), axis=(0, 1), keepdims=True)
     scale = step[0] / jnp.sqrt(total / (rows * count * 2 * n_size * n_size) + 1e-06)
 
-    @pl.loop(0, rows)
-    def _(n):
-        for part in range(2):
-            for h in range(strips):
-                adv[n, part, strip(h)] = own[h][n, part] + scale * der[n, part, strip(h)]
-
-    out_2 = pltpu.make_async_copy(adv, advanced, out_sem.at[1])
-    out_2.start()
+    factor[...] = jnp.broadcast_to(scale[0], factor.shape)
     out.wait()
-    out_2.wait()
 
 
 def smem():
@@ -414,11 +407,11 @@
         piece = vmem((rows, parts, size, n_size), f32)
         held = tuple((piece,) * strips for _ in range(length - 1))
         entries = rows + count * slots + 1
-        return pl.pallas_call(
+        negative, factor = pl.pallas_call(
             functools.partial(kernel, gx, gy, length, strips),
-            out_shape=(jax.ShapeDtypeStruct(state.shape, f32), jax.ShapeDtypeStruct(state.shape, f32)),
+            out_shape=(jax.ShapeDtypeStruct(state.shape, f32), jax.ShapeDtypeStruct((1, n_size), f32)),
             in_specs=[smem()] * 6 + [hbm()] * 4,
-            out_specs=(hbm(), hbm()),
+            out_specs=(hbm(), pl.BlockSpec(memory_space=vmem)),
             scratch_shapes=[
                 (piece,) * strips,
                 held,
@@ -448,9 +441,8 @@
                 vmem((rows * 2 * size, modes * n_size), bf16),
                 vmem((rows * 2 * size, modes * n_size), bf16),
                 vmem(state.shape, f32),
-                vmem(state.shape, f32),
-                vmem((8, n_size), f32),
-                vmem((count, 8, n_size), f32),
+                vmem((1, n_size), f32),
+                vmem((count, 1, n_size), f32),
                 dma((strips,)),
                 dma((strips,)),
                 dma((2,)),
@@ -465,11 +457,12 @@
                 dma((length, strips)),
                 dma((count,)),
                 dma((count,)),
-                dma((2,)),
+                dma((1,)),
             ],
             compiler_params=pltpu.CompilerParams(collective_id=0, has_side_effects=True, vmem_limit_bytes=60 << 20),
             name="step",
         )(up_index, down_index, occupation, bath_coef, bath_rate, step, lists, state, couplings, hamiltonian)
+        return -negative, state - factor[0, 0] * negative
 
     return body
 

time: 100 us -> 98.2 us (0.982)
  other arithmetic: 0 us -> 2.84 us
  local copies, waits for them, and re-layouts: 3.36 us -> 0.56 us
  Pallas kernels: 95.4 us -> 93.3 us
    sub x0 -> x1, other arithmetic: none -> 2.84 us  [body(): return (-negative, state - factor[0, 0] * negative)]
    unnamed x4, local copies, waits for them, and re-layouts: 3.36 us -> 0.56 us
    pallas_call x1, Pallas kernels: 95.4 us -> 93.3 us  [body(): pl.pallas_call(functools.partial(kernel, gx, gy, length, strips), out_sha...]
where the time goes in v2:
time: 98.2 us; the launch traced here: 98 us
  Pallas kernels  93.3 us (95%)
  other arithmetic  2.84 us (3%)
  between operations  1.31 us (1%)
    pallas_call x1, Pallas kernels, body(): pl.pallas_call(functools.partial(kernel, gx, gy, length, strips), out_sha...  93.3 us
    sub x1, other arithmetic, body(): return (-negative, state - factor[0, 0] * negative)  2.84 us

profile of v2, /device:TPU:0, one launch (start us, length us, event | category | flops | bytes accessed | tf_op | source)
XLA Modules:
  0.0 98.0 jit_solution(13225606405817462696)
XLA Ops:
  1.3 0.0 copy-start
  1.3 93.3 %step.2 = (f32[8,2,128,128]{3,2,1,0:T(8,128)}, f32[1,128]{1,0:T(1,128)}) custom-call(s32[8,16]{1,0:T(8,128)} %up.1, s32[8,16]{1,0:T(8,128)} %down.1, s32[8,16]{1,0:T(8,128)} %occ.1, f32[2,16]{1,0:T(2,128)} %coef.1, f32[16]{0:T(128)} %rate.1, f32[1]{0:T(128)S(6)} %copy.12.step, s32[1,1,32]{2,1,0:T(1,128)} %bitcast.4, f32[8,2,128,128]{3,2,1,0:T(8,128)} %state.1, ...), custom_call_target="tpu_custom_call" | custom-call | tf_op jit(solution)/shard_map/step/pallas_call | solution.py:410
  94.6 0.0 copy-start.1
  94.6 0.0 copy-done
  94.6 0.6 copy-done.1
  95.2 2.8 %multiply_subtract_fusion = (f32[8,2,128,128]{3,2,1,0:T(8,128)}, f32[8,2,128,128]{3,2,1,0:T(8,128)}) fusion(f32[8,2,128,128]{3,2,1,0:T(8,128)S(1)} %copy-done, f32[8,2,128,128]{3,2,1,0:T(8,128)} %get-tuple-element.4, f32[]{:T(128)S(1)} %bitcast.3), kind=kLoop, calls=%fused_computation | loop fusion | flops 786432 | bytes 4194308 | tf_op jit(solution)/shard_map/sub | solution.py:465
Async XLA Ops:
  1.3 93.3 %copy-start = (f32[8,2,128,128]{3,2,1,0:T(8,128)S(1)}, f32[8,2,128,128]{3,2,1,0:T(8,128)}, u32[]{:S(2)}) copy-start(f32[8,2,128,128]{3,2,1,0:T(8,128)} %state.1) | copy-start | bytes 3145732
  94.6 0.6 copy-start.1

commit v3 on v2

--- a/solution.py
+++ b/solution.py
@@ -1,4 +1,5 @@
 import functools
+import math
 
 import jax
 import jax.numpy as jnp
@@ -20,12 +21,12 @@
 
 def kernel(
     gx, gy, length, strips,
-    up, down, occ, coef, rate, step, lists, state, couplings, hamiltonian,
+    up_ref, down_ref, occ_ref, coef_ref, rate_ref, step, lists, state, couplings, hamiltonian,
     negative, factor,
-    own, below, above, arrived, stage, list_v, list_s, from_u, from_w, scale_a, scale_b,
+    up, down, occ, coef, rate, own, below, above, arrived, stage, list_v, list_s, from_u, from_w, scale_a, scale_b,
     q_full, q_turned, q_left, q_right, h_full, h_left, h_right, h_x_hi, h_x_lo, h_y,
     x_hi, x_lo, x_hi_2, x_lo_2, y_hi, y_lo, der, squares, gathered,
-    load_sem, copy_sem, q_sem, up_sem, down_sem, below_sem, above_sem, list_send, list_recv, list_load, plane_send, plane_recv,
+    load_sem, copy_sem, q_sem, up_sem, down_sem, below_sem, above_sem, list_up_send, list_up_recv, list_down_send, list_down_recv, list_load, small_sem, near_sem, plane_send, plane_recv,
     sum_send, sum_recv, out_sem,
 ):
     rows, modes = up.shape
@@ -60,20 +61,38 @@
     load_list = pltpu.make_async_copy(lists.at[0], list_s.at[z], list_load.at[0])
     load_list.start()
 
-    for hop in range(1, length):
-        pl.semaphore_signal(barrier, inc=1, device_id=place(column, lax.rem(z + hop, length)), device_id_type=MESH)
-
-    @pl.loop(1, columns)
-    def _(hop):
-        pl.semaphore_signal(barrier, inc=1, device_id=place(lax.rem(column + hop, columns), z), device_id_type=MESH)
-
+    cx, cy = column // side, lax.rem(column, side)
+    line_x = [(lax.rem(cx + hop, gx), y) for hop in range(1, gx)]
+    line_y = [(x, z * side + lax.rem(yy + hop, side)) for hop in range(1, side)]
+    near = line_x + line_y
+
+    def signal(sem, device):
+        pl.semaphore_signal(sem, inc=1, device_id=device, device_id_type=MESH)
+
+    for way in (1, -1):
+
+        @pl.when(jnp.logical_and(z + way >= 0, z + way < length))
+        def _():
+            signal(barrier, place(column, z + way))
+
+    for device in near:
+        signal(barrier, device)
+    smalls = [
+        pltpu.make_async_copy(source, target, small_sem.at[i])
+        for i, (source, target) in enumerate(
+            ((up_ref, up), (down_ref, down), (occ_ref, occ), (coef_ref, coef), (rate_ref, rate))
+        )
+    ]
+    for copy in smalls:
+        copy.start()
     for h in range(strips):
         load_again(h).start()
     load_q = pltpu.make_async_copy(couplings, q_full, q_sem.at[0])
     load_h = pltpu.make_async_copy(hamiltonian, h_full, q_sem.at[1])
     load_q.start()
     load_h.start()
-    pl.semaphore_wait(barrier, length + columns - 2)
+    level_peers = jnp.where(z > 0, 1, 0) + jnp.where(z + 1 < length, 1, 0)
+    pl.semaphore_wait(barrier, len(near) + level_peers)
 
     def relay(hop, h, way):
         held = below if way > 0 else above
@@ -86,18 +105,27 @@
             device_id_type=MESH,
         )
 
-    def send_lists(hop):
+    def send_list(hop, way):
+        level = z - way * hop
         return pltpu.make_async_remote_copy(
-            src_ref=lists.at[0],
-            dst_ref=list_v.at[z],
-            send_sem=list_send.at[hop],
-            recv_sem=list_recv.at[hop],
-            device_id=place(column, lax.rem(z + hop, length)),
+            src_ref=list_v.at[level] if hop else lists.at[0],
+            dst_ref=list_v.at[level],
+            send_sem=(list_up_send if way > 0 else list_down_send).at[hop],
+            recv_sem=(list_up_recv if way > 0 else list_down_recv).at[hop],
+            device_id=place(column, z + way),
             device_id_type=MESH,
         )
 
-    for hop in range(1, length):
-        send_lists(hop).start()
+    def goes(hop, way):
+        level = z - way * hop
+        return jnp.logical_and(jnp.logical_and(level >= 0, level < length), jnp.logical_and(z + way >= 0, z + way < length))
+
+    for way in (1, -1):
+
+        @pl.when(goes(0, way))
+        def _():
+            send_list(0, way).start()
+
     for h in range(strips):
         load(h).wait()
 
@@ -109,7 +137,10 @@
         def _():
             relay(0, h, -1).start()
 
+    for device in near:
+        signal(near_sem.at[0], device)
     load_list.wait()
+    pl.semaphore_wait(near_sem.at[0], len(near))
 
     def hand(level, h, hop, slot):
         return pltpu.make_async_remote_copy(
@@ -152,8 +183,35 @@
     for h in range(strips):
         distribute(own[h], z, h)
 
+    def take_list(hop, way):
+        level = z - way * hop
+
+        @pl.when(jnp.logical_and(level >= 0, level < length))
+        def _():
+            copy = pltpu.make_async_remote_copy(
+                src_ref=lists.at[0],
+                dst_ref=list_v.at[level],
+                send_sem=(list_up_send if way > 0 else list_down_send).at[hop - 1],
+                recv_sem=(list_up_recv if way > 0 else list_down_recv).at[hop - 1],
+                device_id=place(column, z),
+                device_id_type=MESH,
+            )
+            copy.wait_recv()
+            if hop + 1 < length:
+
+                @pl.when(goes(hop, way))
+                def _():
+                    send_list(hop, way).start()
+
+            move = pltpu.make_async_copy(list_v.at[level], list_s.at[level], list_load.at[1])
+            move.start()
+            move.wait()
+
     def arrive(hop, h):
         low, high = z - hop, z + hop
+        if h == 0:
+            take_list(hop, 1)
+            take_list(hop, -1)
 
         @pl.when(low >= 0)
         def _():
@@ -181,16 +239,10 @@
         def _():
             distribute(above[hop - 1][h], high, h)
 
-    for hop in range(1, length):
-        send_lists(hop).wait()
-    for hop in range(1, length):
-        level = lax.rem(z + hop, length)
-        copy = pltpu.make_async_copy(list_v.at[level], list_s.at[level], list_load.at[hop])
-        copy.start()
-        copy.wait()
-
     load_q.wait()
     load_h.wait()
+    for copy in smalls:
+        copy.wait()
     for k in range(modes):
         high, low = split(q_full[k])
         at = pl.ds(k * n_size, n_size)
@@ -356,6 +408,12 @@
             all_hands(level, h).wait_send()
 
     for hop in range(length - 1):
+        for way in (1, -1):
+
+            @pl.when(goes(hop, way))
+            def _():
+                send_list(hop, way).wait_send()
+
         for h in range(strips):
 
             @pl.when(jnp.logical_and(z >= hop, z + 1 < length))
@@ -377,12 +435,8 @@
     out.wait()
 
 
-def smem():
-    return pl.BlockSpec(memory_space=pltpu.SMEM)
-
-
-def hbm():
-    return pl.BlockSpec(memory_space=pl.ANY)
+def hbm(array):
+    return pltpu.with_memory_space_constraint(array, pltpu.HBM)
 
 
 def line_length(gx, gy):
@@ -403,65 +457,84 @@
         size = n_size // strips
         lists = jnp.swapaxes(send_list, 1, 2)
         f32, bf16, i32 = jnp.float32, jnp.bfloat16, jnp.int32
-        vmem, sm, dma = pltpu.VMEM, pltpu.SMEM, pltpu.SemaphoreType.DMA
-        piece = vmem((rows, parts, size, n_size), f32)
-        held = tuple((piece,) * strips for _ in range(length - 1))
+        sm, dma = pltpu.SMEM, pltpu.SemaphoreType.DMA
+        used = []
+
+        def vmem(shape, dtype, copies=1):
+            used.append(math.prod(shape) * jnp.dtype(dtype).itemsize * copies)
+            return pltpu.VMEM(shape, dtype)
+
+        def tuple_of(shape, dtype, copies):
+            return (vmem(shape, dtype, copies),) * copies
+
+        piece = (rows, parts, size, n_size)
+        held = [tuple(tuple_of(piece, f32, strips) for _ in range(length - 1)) for _ in range(2)]
         entries = rows + count * slots + 1
+        scratch = [
+            sm(up_index.shape, i32),
+            sm(down_index.shape, i32),
+            sm(occupation.shape, i32),
+            sm(bath_coef.shape, f32),
+            sm(bath_rate.shape, f32),
+            tuple_of(piece, f32, strips),
+            *held,
+            tuple_of((entries, parts, size, n_size), f32, strips),
+            vmem((length, strips, columns * slots, parts, size, n_size), f32),
+            vmem((length, slots, count), i32),
+            sm((length, slots, count), i32),
+            sm((rows, modes), i32),
+            sm((rows, modes), i32),
+            sm((rows, modes), f32),
+            sm((rows, modes), f32),
+            vmem(couplings.shape, f32),
+            vmem(couplings.shape, f32),
+            vmem((strips, 2 * n_size, modes * size), bf16),
+            vmem((modes * n_size, 2 * n_size), bf16),
+            vmem(hamiltonian.shape, f32),
+            vmem((2 * n_size, 2 * n_size), bf16),
+            vmem((2 * n_size, 2 * n_size), bf16),
+            vmem((2 * n_size, 2 * n_size), bf16),
+            vmem((2 * n_size, 2 * n_size), bf16),
+            vmem((4 * n_size, 2 * n_size), bf16),
+            vmem((modes * size, 2 * n_size), bf16),
+            vmem((modes * size, 2 * n_size), bf16),
+            vmem((modes * size, 2 * n_size), bf16),
+            vmem((modes * size, 2 * n_size), bf16),
+            vmem((rows * 2 * size, modes * n_size), bf16),
+            vmem((rows * 2 * size, modes * n_size), bf16),
+            vmem(state.shape, f32),
+            vmem((1, n_size), f32),
+            vmem((count, 1, n_size), f32),
+            dma((strips,)),
+            dma((strips,)),
+            dma((2,)),
+            dma((length, strips)),
+            dma((length, strips)),
+            dma((length, strips)),
+            dma((length, strips)),
+            dma((length,)),
+            dma((length,)),
+            dma((length,)),
+            dma((length,)),
+            dma((2,)),
+            dma((5,)),
+            pltpu.SemaphoreType.REGULAR((1,)),
+            dma((length, strips)),
+            dma((length, strips)),
+            dma((count,)),
+            dma((count,)),
+            dma((1,)),
+        ]
+        grant = min(sum(used) + (6 << 20), 60 << 20)
         negative, factor = pl.pallas_call(
             functools.partial(kernel, gx, gy, length, strips),
             out_shape=(jax.ShapeDtypeStruct(state.shape, f32), jax.ShapeDtypeStruct((1, n_size), f32)),
-            in_specs=[smem()] * 6 + [hbm()] * 4,
-            out_specs=(hbm(), pl.BlockSpec(memory_space=vmem)),
-            scratch_shapes=[
-                (piece,) * strips,
-                held,
-                held,
-                (vmem((entries, parts, size, n_size), f32),) * strips,
-                vmem((length, strips, columns * slots, parts, size, n_size), f32),
-                vmem((length, slots, count), i32),
-                sm((length, slots, count), i32),
-                sm((rows, modes), i32),
-                sm((rows, modes), i32),
-                sm((rows, modes), f32),
-                sm((rows, modes), f32),
-                vmem(couplings.shape, f32),
-                vmem(couplings.shape, f32),
-                vmem((strips, 2 * n_size, modes * size), bf16),
-                vmem((modes * n_size, 2 * n_size), bf16),
-                vmem(hamiltonian.shape, f32),
-                vmem((2 * n_size, 2 * n_size), bf16),
-                vmem((2 * n_size, 2 * n_size), bf16),
-                vmem((2 * n_size, 2 * n_size), bf16),
-                vmem((2 * n_size, 2 * n_size), bf16),
-                vmem((4 * n_size, 2 * n_size), bf16),
-                vmem((modes * size, 2 * n_size), bf16),
-                vmem((modes * size, 2 * n_size), bf16),
-                vmem((modes * size, 2 * n_size), bf16),
-                vmem((modes * size, 2 * n_size), bf16),
-                vmem((rows * 2 * size, modes * n_size), bf16),
-                vmem((rows * 2 * size, modes * n_size), bf16),
-                vmem(state.shape, f32),
-                vmem((1, n_size), f32),
-                vmem((count, 1, n_size), f32),
-                dma((strips,)),
-                dma((strips,)),
-                dma((2,)),
-                dma((length, strips)),
-                dma((length, strips)),
-                dma((length, strips)),
-                dma((length, strips)),
-                dma((length,)),
-                dma((length,)),
-                dma((length,)),
-                dma((length, strips)),
-                dma((length, strips)),
-                dma((count,)),
-                dma((count,)),
-                dma((1,)),
-            ],
-            compiler_params=pltpu.CompilerParams(collective_id=0, has_side_effects=True, vmem_limit_bytes=60 << 20),
+            in_specs=[pl.BlockSpec(memory_space=pltpu.HBM)] * 5 + [pl.BlockSpec(memory_space=pltpu.SMEM)] + [pl.BlockSpec(memory_space=pltpu.HBM)] * 4,
+            out_specs=(pl.BlockSpec(memory_space=pl.ANY), pl.BlockSpec(memory_space=pltpu.VMEM)),
+            scratch_shapes=scratch,
+            compiler_params=pltpu.CompilerParams(collective_id=0, has_side_effects=True, vmem_limit_bytes=grant),
             name="step",
-        )(up_index, down_index, occupation, bath_coef, bath_rate, step, lists, state, couplings, hamiltonian)
+        )(*(hbm(a) for a in (up_index, down_index, occupation, bath_coef, bath_rate)), step, *(hbm(a) for a in (lists, state, couplings, hamiltonian)))
         return -negative, state - factor[0, 0] * negative
 
     return body

time: 98.2 us -> 95.1 us (0.968)
  other arithmetic: 2.84 us -> 1.57 us
  Pallas kernels: 93.3 us -> 92.1 us
    sub x1, other arithmetic: 2.84 us -> 1.57 us  [body(): return (-negative, state - factor[0, 0] * negative)]
    pallas_call x1, Pallas kernels: 93.3 us -> 92.1 us  [body(): pl.pallas_call(functools.partial(kernel, gx, gy, length, strips), out_sha...]
where the time goes in v3:
time: 95.1 us; the launch traced here: 95 us
  Pallas kernels  92.1 us (97%)
  other arithmetic  1.57 us (2%)
  between operations  1.3 us (1%)
    pallas_call x1, Pallas kernels, body(): pl.pallas_call(functools.partial(kernel, gx, gy, length, strips), out_sha...  92.1 us

profile of v3, /device:TPU:0, one launch (start us, length us, event | category | flops | bytes accessed | tf_op | source)
XLA Modules:
  0.0 95.0 jit_solution(7385952062784396641)
XLA Ops:
  1.3 0.0 copy-start
  1.3 92.1 %step.2 = (f32[8,2,128,128]{3,2,1,0:T(8,128)S(1)}, f32[1,128]{1,0:T(1,128)S(1)}) custom-call(s32[8,16]{1,0:T(8,128)} %up_ref.1, s32[8,16]{1,0:T(8,128)} %down_ref.1, s32[8,16]{1,0:T(8,128)} %occ_ref.1, f32[2,16]{1,0:T(2,128)} %coef_ref.1, f32[16]{0:T(128)} %rate_ref.1, f32[1]{0:T(128)S(6)} %copy.12.step, s32[1,1,32]{2,1,0:T(1,128)} %bitcast.4, ...), custom_call_target="tpu_custom_call" | custom-call | tf_op jit(solution)/shard_map/step/pallas_call | solution.py:529
  93.4 0.0 copy-done
  93.4 1.6 %multiply_subtract_fusion = (f32[8,2,128,128]{3,2,1,0:T(8,128)}, f32[8,2,128,128]{3,2,1,0:T(8,128)}) fusion(f32[8,2,128,128]{3,2,1,0:T(8,128)S(1)} %copy-done, f32[8,2,128,128]{3,2,1,0:T(8,128)S(1)} %get-tuple-element.4, f32[]{:T(128)S(1)} %bitcast.3), kind=kLoop, calls=%fused_computation | loop fusion | flops 786432 | bytes 4194308 | tf_op jit(solution)/shard_map/sub | solution.py:538
Async XLA Ops:
  1.3 92.1 %copy-start = (f32[8,2,128,128]{3,2,1,0:T(8,128)S(1)}, f32[8,2,128,128]{3,2,1,0:T(8,128)}, u32[]{:S(2)}) copy-start(f32[8,2,128,128]{3,2,1,0:T(8,128)} %state.1) | copy-start | bytes 3145732

commit v4 on v3

--- a/solution.py
+++ b/solution.py
@@ -25,7 +25,7 @@
     negative, factor,
     up, down, occ, coef, rate, own, below, above, arrived, stage, list_v, list_s, from_u, from_w, scale_a, scale_b,
     q_full, q_turned, q_left, q_right, h_full, h_left, h_right, h_x_hi, h_x_lo, h_y,
-    x_hi, x_lo, x_hi_2, x_lo_2, y_hi, y_lo, der, squares, gathered,
+    sets, der, squares, gathered,
     load_sem, copy_sem, q_sem, up_sem, down_sem, below_sem, above_sem, list_up_send, list_up_recv, list_down_send, list_down_recv, list_load, small_sem, near_sem, plane_send, plane_recv,
     sum_send, sum_recv, out_sem,
 ):
@@ -36,6 +36,7 @@
     columns = gx * side
     slots = lists.shape[1]
     size = n_size // strips
+    lane = q_left.shape[3]
     x, y = lax.axis_index("gx"), lax.axis_index("gy")
     me = x * gy + y
     z, yy = y // side, lax.rem(y, side)
@@ -246,8 +247,8 @@
     for k in range(modes):
         high, low = split(q_full[k])
         at = pl.ds(k * n_size, n_size)
-        q_right[at, pl.ds(0, n_size)] = high
-        q_right[at, pl.ds(n_size, n_size)] = low
+        q_right[0, at, :] = high
+        q_right[1, at, :] = low
         q_turned[k] = q_full[k].T
     for k in range(2):
         high, low = split(h_full[k])
@@ -263,8 +264,10 @@
     for h in range(strips):
         turned = q_turned[:, h * size:(h + 1) * size, :].reshape(modes * size, n_size).T
         high, low = split(turned)
-        q_left[h, pl.ds(0, n_size), :] = high
-        q_left[h, pl.ds(n_size, n_size), :] = low
+        for tile in range(q_left.shape[1]):
+            lanes = slice(tile * lane, (tile + 1) * lane)
+            q_left[h, tile, pl.ds(0, n_size), :] = high[:, lanes]
+            q_left[h, tile, pl.ds(n_size, n_size), :] = low[:, lanes]
 
     empty = rows + count * slots
 
@@ -321,7 +324,8 @@
         for h in range(strips):
             arrive(hop, h)
 
-    def build(h, n, xh, xl):
+    def build(h, n, place_y, held):
+        (xh, xl), y_held = held[0][place_y], held[1]
         source = arrived[h]
         for k in range(modes):
             iu, iw = from_u[n, k], from_w[n, k]
@@ -332,35 +336,43 @@
             r, s = ui + a * wi, b * wr
             at = pl.ds(k * size, size)
             for part, value in enumerate((p - q, r + s)):
-                lanes = pl.ds(part * n_size, n_size)
-                xh[at, lanes], xl[at, lanes] = split(value)
+                xh[part, at, :], xl[part, at, :] = split(value)
             for part, value in enumerate((p + q, r - s)):
-                at_y = pl.ds(pl.multiple_of((n * 2 + part) * size, size), size)
-                lanes = pl.ds(k * n_size, n_size)
-                y_hi[at_y, lanes], y_lo[at_y, lanes] = split(value)
+                for level, piece in enumerate(split(value)):
+                    y_held[k, pl.ds((place_y * 4 + level * 2 + part) * size, size), :] = piece
+
+    def wide(parts):
+        return jnp.concatenate(parts, axis=1)
 
     def finish(h, n, xh, xl):
-        both = dot(q_left[h], xh[...])
-        left = both[:n_size] + both[n_size:] + dot(q_left[h, :n_size, :], xl[...])
+        matrix = wide([q_left[h, tile] for tile in range(q_left.shape[1])])
+        both = dot(matrix, wide([xh[0], xh[1]]))
+        left = both[:n_size] + both[n_size:] + dot(matrix[:n_size], wide([xl[0], xl[1]]))
         der[n, 0] -= left[:, n_size:]
         der[n, 1] += left[:, :n_size]
 
+    def finish_right(h, first, held):
+        product = dot(wide([held[k] for k in range(modes)]), wide([q_right[0], q_right[1]]))
+        for n in range(2):
+            re, im, re_lo, im_lo = (product[(4 * n + i) * size:(4 * n + i + 1) * size] for i in range(4))
+            der[first + n, 0, strip(h)] += im[:, :n_size] + (im[:, n_size:] + im_lo[:, :n_size])
+            der[first + n, 1, strip(h)] -= re[:, :n_size] + (re[:, n_size:] + re_lo[:, :n_size])
+
     def compute(h):
-        build(h, 0, x_hi, x_lo)
-
-        @pl.loop(0, rows // 2)
-        def _(pair):
-            n = pair * 2
-            build(h, n + 1, x_hi_2, x_lo_2)
-            finish(h, n, x_hi, x_lo)
-            build(h, jnp.minimum(n + 2, rows - 2), x_hi, x_lo)
-            finish(h, n + 1, x_hi_2, x_lo_2)
-
-        high = dot(y_hi[...], q_right[...])
-        right = high[:, :n_size] + high[:, n_size:] + dot(y_lo[...], q_right[:, :n_size])
-        for n in range(rows):
-            der[n, 0, strip(h)] += right[(2 * n + 1) * size:(2 * n + 2) * size]
-            der[n, 1, strip(h)] -= right[2 * n * size:(2 * n + 1) * size]
+        for n in range(2):
+            build(h, n, n, sets[0])
+
+        def stage(first, held, coming):
+            finish_right(h, first, held[1])
+            for n in range(2):
+                finish(h, first + n, *held[0][n])
+            for n in range(2):
+                build(h, jnp.minimum(first + 2, rows - 2) + n, n, coming)
+
+        @pl.loop(0, rows // 4)
+        def _(four):
+            stage(four * 4, sets[0], sets[1])
+            stage(four * 4 + 2, sets[1], sets[0])
 
     def process(h):
         for level in range(length):
@@ -455,6 +467,7 @@
         slots = send_list.shape[2]
         strips = 8 if n_size % 128 == 0 else 1
         size = n_size // strips
+        lane = math.gcd(modes * size, 128)
         lists = jnp.swapaxes(send_list, 1, 2)
         f32, bf16, i32 = jnp.float32, jnp.bfloat16, jnp.int32
         sm, dma = pltpu.SMEM, pltpu.SemaphoreType.DMA
@@ -488,20 +501,18 @@
             sm((rows, modes), f32),
             vmem(couplings.shape, f32),
             vmem(couplings.shape, f32),
-            vmem((strips, 2 * n_size, modes * size), bf16),
-            vmem((modes * n_size, 2 * n_size), bf16),
+            vmem((strips, modes * size // lane, 2 * n_size, lane), bf16),
+            vmem((2, modes * n_size, n_size), bf16),
             vmem(hamiltonian.shape, f32),
             vmem((2 * n_size, 2 * n_size), bf16),
             vmem((2 * n_size, 2 * n_size), bf16),
             vmem((2 * n_size, 2 * n_size), bf16),
             vmem((2 * n_size, 2 * n_size), bf16),
             vmem((4 * n_size, 2 * n_size), bf16),
-            vmem((modes * size, 2 * n_size), bf16),
-            vmem((modes * size, 2 * n_size), bf16),
-            vmem((modes * size, 2 * n_size), bf16),
-            vmem((modes * size, 2 * n_size), bf16),
-            vmem((rows * 2 * size, modes * n_size), bf16),
-            vmem((rows * 2 * size, modes * n_size), bf16),
+            tuple(
+                (tuple(tuple_of((2, modes * size, n_size), bf16, 2) for _ in range(2)), vmem((modes, 8 * size, n_size), bf16))
+                for _ in range(2)
+            ),
             vmem(state.shape, f32),
             vmem((1, n_size), f32),
             vmem((count, 1, n_size), f32),

time: 95.1 us -> 91.5 us (0.962)
  Pallas kernels: 92.1 us -> 88.5 us
    pallas_call x1, Pallas kernels: 92.1 us -> 88.5 us  [body(): pl.pallas_call(functools.partial(kernel, gx, gy, length, strips), out_sha...]
where the time goes in v4:
time: 91.5 us; the launch traced here: 91.3 us
  Pallas kernels  88.5 us (97%)
  other arithmetic  1.57 us (2%)
  between operations  1.3 us (1%)
    pallas_call x1, Pallas kernels, body(): pl.pallas_call(functools.partial(kernel, gx, gy, length, strips), out_sha...  88.5 us

profile of v4, /device:TPU:0, one launch (start us, length us, event | category | flops | bytes accessed | tf_op | source)
XLA Modules:
  0.0 91.3 jit_solution(124736848183344275)
XLA Ops:
  1.3 0.0 copy-start
  1.3 88.5 %step.2 = (f32[8,2,128,128]{3,2,1,0:T(8,128)S(1)}, f32[1,128]{1,0:T(1,128)S(1)}) custom-call(s32[8,16]{1,0:T(8,128)} %up_ref.1, s32[8,16]{1,0:T(8,128)} %down_ref.1, s32[8,16]{1,0:T(8,128)} %occ_ref.1, f32[2,16]{1,0:T(2,128)} %coef_ref.1, f32[16]{0:T(128)} %rate_ref.1, f32[1]{0:T(128)S(6)} %copy.12.step, s32[1,1,32]{2,1,0:T(1,128)} %bitcast.4, ...), custom_call_target="tpu_custom_call" | custom-call | tf_op jit(solution)/shard_map/step/pallas_call | solution.py:540
  89.8 0.0 copy-done
  89.8 1.6 %multiply_subtract_fusion = (f32[8,2,128,128]{3,2,1,0:T(8,128)}, f32[8,2,128,128]{3,2,1,0:T(8,128)}) fusion(f32[8,2,128,128]{3,2,1,0:T(8,128)S(1)} %copy-done, f32[8,2,128,128]{3,2,1,0:T(8,128)S(1)} %get-tuple-element.4, f32[]{:T(128)S(1)} %bitcast.3), kind=kLoop, calls=%fused_computation | loop fusion | flops 786432 | bytes 4194308 | tf_op jit(solution)/shard_map/sub | solution.py:549
Async XLA Ops:
  1.3 88.5 %copy-start = (f32[8,2,128,128]{3,2,1,0:T(8,128)S(1)}, f32[8,2,128,128]{3,2,1,0:T(8,128)}, u32[]{:S(2)}) copy-start(f32[8,2,128,128]{3,2,1,0:T(8,128)} %state.1) | copy-start | bytes 3145732

commit v5 on v4

--- a/solution.py
+++ b/solution.py
@@ -20,14 +20,14 @@
 
 
 def kernel(
-    gx, gy, length, strips,
+    gx, gy, length, strips, direct,
     up_ref, down_ref, occ_ref, coef_ref, rate_ref, step, lists, state, couplings, hamiltonian,
     negative, factor,
     up, down, occ, coef, rate, own, below, above, arrived, stage, list_v, list_s, from_u, from_w, scale_a, scale_b,
     q_full, q_turned, q_left, q_right, h_full, h_left, h_right, h_x_hi, h_x_lo, h_y,
-    sets, der, squares, gathered,
+    sets, der, squares, gathered, straight,
     load_sem, copy_sem, q_sem, up_sem, down_sem, below_sem, above_sem, list_up_send, list_up_recv, list_down_send, list_down_recv, list_load, small_sem, near_sem, plane_send, plane_recv,
-    sum_send, sum_recv, out_sem,
+    sum_send, sum_recv, out_sem, straight_send,
 ):
     rows, modes = up.shape
     n_size = state.shape[2]
@@ -43,6 +43,8 @@
     column = x * side + yy
     dot = functools.partial(jnp.dot, preferred_element_type=jnp.float32)
 
+    last = length - 1
+
     def place(at, level):
         return at // side, level * side + lax.rem(at, side)
 
@@ -142,6 +144,8 @@
         signal(near_sem.at[0], device)
     load_list.wait()
     pl.semaphore_wait(near_sem.at[0], len(near))
+    for device in near:
+        signal(near_sem.at[1], device)
 
     def hand(level, h, hop, slot):
         return pltpu.make_async_remote_copy(
@@ -164,8 +168,8 @@
             device_id_type=MESH,
         )
 
-    def chosen(held, level, at, slot):
-        target = place(at, z)
+    def chosen(held, level, at, slot, to=None):
+        target = place(at, z if to is None else to)
         pick = list_s[level, slot, target[0] * gy + target[1]]
         keep = jnp.where(pick < 0, 0.0, 1.0).astype(jnp.float32)
         pick = jnp.clip(pick, 0, rows - 1)
@@ -183,6 +187,32 @@
 
     for h in range(strips):
         distribute(own[h], z, h)
+
+    def send_straight(held, level, h, way):
+        for slot in range(slots):
+
+            @pl.loop(0, columns)
+            def _(hop):
+                at = lax.rem(column + hop, columns)
+                straight[h, hop * slots + slot] = chosen(held, level, at, slot, z + way)
+                pltpu.make_async_remote_copy(
+                    src_ref=straight.at[h, hop * slots + slot],
+                    dst_ref=arrived[h].at[rows + (level * columns + hop) * slots + slot],
+                    send_sem=straight_send.at[h],
+                    recv_sem=plane_recv.at[level, h],
+                    device_id=place(at, z + way),
+                    device_id_type=MESH,
+                ).start()
+
+    def straight_waits(level, h):
+        return pltpu.make_async_remote_copy(
+            src_ref=straight.at[h],
+            dst_ref=arrived[h].at[pl.ds(rows + level * columns * slots, columns * slots)],
+            send_sem=straight_send.at[h],
+            recv_sem=plane_recv.at[level, h],
+            device_id=place(lax.rem(column + 1, columns), z),
+            device_id_type=MESH,
+        )
 
     def take_list(hop, way):
         level = z - way * hop
@@ -214,31 +244,28 @@
             take_list(hop, 1)
             take_list(hop, -1)
 
-        @pl.when(low >= 0)
-        def _():
-            relay(hop - 1, h, 1).wait_recv()
-            if hop + 1 < length:
-
-                @pl.when(z + 1 < length)
-                def _():
-                    relay(hop, h, 1).start()
-
-        @pl.when(high < length)
-        def _():
-            relay(hop - 1, h, -1).wait_recv()
-            if hop + 1 < length:
-
-                @pl.when(z > 0)
-                def _():
-                    relay(hop, h, -1).start()
-
-        @pl.when(low >= 0)
-        def _():
-            distribute(below[hop - 1][h], low, h)
-
-        @pl.when(high < length)
-        def _():
-            distribute(above[hop - 1][h], high, h)
+        if direct and hop == last:
+            return
+        ways = ((1, low, below), (-1, high, above))
+        for way, level, held in ways:
+
+            @pl.when(jnp.logical_and(level >= 0, level < length))
+            def _():
+                relay(hop - 1, h, way).wait_recv()
+                if hop + 1 < length:
+
+                    @pl.when(goes(hop, way))
+                    def _():
+                        if direct and hop == last - 1:
+                            send_straight(held[hop - 1][h], level, h, way)
+                        else:
+                            relay(hop, h, way).start()
+
+        for way, level, held in ways:
+
+            @pl.when(jnp.logical_and(level >= 0, level < length))
+            def _():
+                distribute(held[hop - 1][h], level, h)
 
     load_q.wait()
     load_h.wait()
@@ -320,6 +347,7 @@
             der[n, 0, strip(h)] = damping * own[h][n, 0] - im[at]
             der[n, 1, strip(h)] = damping * own[h][n, 1] + re[at]
 
+    pl.semaphore_wait(near_sem.at[1], len(near))
     for hop in range(2, length - 1):
         for h in range(strips):
             arrive(hop, h)
@@ -376,14 +404,23 @@
 
     def process(h):
         for level in range(length):
-            all_hands(level, h).wait_recv()
+            if direct and level in (0, last):
+
+                @pl.when(z == last - level)
+                def _():
+                    straight_waits(level, h).wait_recv()
+
+                @pl.when(z != last - level)
+                def _():
+                    all_hands(level, h).wait_recv()
+            else:
+                all_hands(level, h).wait_recv()
         if COMPUTE:
             compute(h)
 
     for h in range(strips):
         load_again(h).wait()
 
-    last = length - 1
     for h in range(strips):
         arrive(last, h)
         if h:
@@ -402,8 +439,8 @@
         return pltpu.make_async_remote_copy(
             src_ref=squares,
             dst_ref=gathered.at[hop],
-            send_sem=sum_send.at[hop],
-            recv_sem=sum_recv.at[hop],
+            send_sem=sum_send.at[0],
+            recv_sem=sum_recv.at[0],
             device_id=(other // gy, lax.rem(other, gy)),
             device_id_type=MESH,
         )
@@ -417,7 +454,17 @@
     gathered[0] = squares[...]
     for level in range(length):
         for h in range(strips):
-            all_hands(level, h).wait_send()
+            if direct and level in (0, last):
+
+                @pl.when(z != last - level)
+                def _():
+                    all_hands(level, h).wait_send()
+
+                @pl.when(z == (last - 1 if level == 0 else 1))
+                def _():
+                    straight_waits(level, h).wait_send()
+            else:
+                all_hands(level, h).wait_send()
 
     for hop in range(length - 1):
         for way in (1, -1):
@@ -425,20 +472,21 @@
             @pl.when(goes(hop, way))
             def _():
                 send_list(hop, way).wait_send()
-
-        for h in range(strips):
-
-            @pl.when(jnp.logical_and(z >= hop, z + 1 < length))
-            def _():
-                relay(hop, h, 1).wait_send()
-
-            @pl.when(jnp.logical_and(z + hop < length, z > 0))
-            def _():
-                relay(hop, h, -1).wait_send()
-
-    @pl.loop(1, count)
-    def _(hop):
-        copy_to(hop).wait()
+                if not (direct and hop == last - 1):
+                    for h in range(strips):
+                        relay(hop, h, way).wait_send()
+
+    others = pl.ds(1, count - 1)
+    sums = pltpu.make_async_remote_copy(
+        src_ref=gathered.at[others],
+        dst_ref=gathered.at[others],
+        send_sem=sum_send.at[0],
+        recv_sem=sum_recv.at[0],
+        device_id=place(lax.rem(column + 1, columns), z),
+        device_id_type=MESH,
+    )
+    sums.wait_send()
+    sums.wait_recv()
 
     total = jnp.sum(jnp.sum(gathered[...], axis=0), axis=(0, 1), keepdims=True)
     scale = step[0] / jnp.sqrt(total / (rows * count * 2 * n_size * n_size) + 1e-06)
@@ -483,6 +531,8 @@
         piece = (rows, parts, size, n_size)
         held = [tuple(tuple_of(piece, f32, strips) for _ in range(length - 1)) for _ in range(2)]
         entries = rows + count * slots + 1
+        direct = length >= 4 and columns * slots <= rows
+        few = columns * slots if direct else 1
         scratch = [
             sm(up_index.shape, i32),
             sm(down_index.shape, i32),
@@ -516,6 +566,7 @@
             vmem(state.shape, f32),
             vmem((1, n_size), f32),
             vmem((count, 1, n_size), f32),
+            vmem((strips, few, parts, size, n_size) if direct else (1, 1, 1, 8, n_size), f32),
             dma((strips,)),
             dma((strips,)),
             dma((2,)),
@@ -529,16 +580,17 @@
             dma((length,)),
             dma((2,)),
             dma((5,)),
-            pltpu.SemaphoreType.REGULAR((1,)),
+            pltpu.SemaphoreType.REGULAR((2,)),
             dma((length, strips)),
             dma((length, strips)),
-            dma((count,)),
-            dma((count,)),
             dma((1,)),
+            dma((1,)),
+            dma((1,)),
+            dma((strips,)),
         ]
         grant = min(sum(used) + (6 << 20), 60 << 20)
         negative, factor = pl.pallas_call(
-            functools.partial(kernel, gx, gy, length, strips),
+            functools.partial(kernel, gx, gy, length, strips, direct),
             out_shape=(jax.ShapeDtypeStruct(state.shape, f32), jax.ShapeDtypeStruct((1, n_size), f32)),
             in_specs=[pl.BlockSpec(memory_space=pltpu.HBM)] * 5 + [pl.BlockSpec(memory_space=pltpu.SMEM)] + [pl.BlockSpec(memory_space=pltpu.HBM)] * 4,
             out_specs=(pl.BlockSpec(memory_space=pl.ANY), pl.BlockSpec(memory_space=pltpu.VMEM)),

time: 91.5 us -> 86.9 us (0.950)
  Pallas kernels: 88.5 us -> 83.9 us
    pallas_call x1, Pallas kernels: 88.5 us -> 83.9 us  [body(): pl.pallas_call(functools.partial(kernel, gx, gy, length, strips, direct),...]
where the time goes in v5:
time: 86.9 us; the launch traced here: 86.7 us
  Pallas kernels  83.9 us (97%)
  other arithmetic  1.57 us (2%)
  between operations  1.3 us (1%)
    pallas_call x1, Pallas kernels, body(): pl.pallas_call(functools.partial(kernel, gx, gy, length, strips, direct),...  83.9 us

profile of v5, /device:TPU:0, one launch (start us, length us, event | category | flops | bytes accessed | tf_op | source)
XLA Modules:
  0.0 86.7 jit_solution(3116143148302090670)
XLA Ops:
  1.3 0.0 copy-start
  1.3 83.9 %step.2 = (f32[8,2,128,128]{3,2,1,0:T(8,128)S(1)}, f32[1,128]{1,0:T(1,128)S(1)}) custom-call(s32[8,16]{1,0:T(8,128)} %up_ref.1, s32[8,16]{1,0:T(8,128)} %down_ref.1, s32[8,16]{1,0:T(8,128)} %occ_ref.1, f32[2,16]{1,0:T(2,128)} %coef_ref.1, f32[16]{0:T(128)} %rate_ref.1, f32[1]{0:T(128)S(6)} %copy.12.step, s32[1,1,32]{2,1,0:T(1,128)} %bitcast.4, ...), custom_call_target="tpu_custom_call" | custom-call | tf_op jit(solution)/shard_map/step/pallas_call | solution.py:592
  85.2 0.0 copy-done
  85.2 1.6 %multiply_subtract_fusion = (f32[8,2,128,128]{3,2,1,0:T(8,128)}, f32[8,2,128,128]{3,2,1,0:T(8,128)}) fusion(f32[8,2,128,128]{3,2,1,0:T(8,128)S(1)} %copy-done, f32[8,2,128,128]{3,2,1,0:T(8,128)S(1)} %get-tuple-element.4, f32[]{:T(128)S(1)} %bitcast.3), kind=kLoop, calls=%fused_computation | loop fusion | flops 786432 | bytes 4194308 | tf_op jit(solution)/shard_map/sub | solution.py:601
Async XLA Ops:
  1.3 83.9 %copy-start = (f32[8,2,128,128]{3,2,1,0:T(8,128)S(1)}, f32[8,2,128,128]{3,2,1,0:T(8,128)}, u32[]{:S(2)}) copy-start(f32[8,2,128,128]{3,2,1,0:T(8,128)} %state.1) | copy-start | bytes 3145732

commit v6 on v5

--- a/solution.py
+++ b/solution.py
@@ -25,7 +25,7 @@
     negative, factor,
     up, down, occ, coef, rate, own, below, above, arrived, stage, list_v, list_s, from_u, from_w, scale_a, scale_b,
     q_full, q_turned, q_left, q_right, h_full, h_left, h_right, h_x_hi, h_x_lo, h_y,
-    sets, der, squares, gathered, straight,
+    sets, der, squares, gathered, straight, partial,
     load_sem, copy_sem, q_sem, up_sem, down_sem, below_sem, above_sem, list_up_send, list_up_recv, list_down_send, list_down_recv, list_load, small_sem, near_sem, plane_send, plane_recv,
     sum_send, sum_recv, out_sem, straight_send,
 ):
@@ -59,10 +59,6 @@
     def load_again(h):
         return pltpu.make_async_copy(state.at[:, :, strip(h)], arrived[h].at[pl.ds(0, rows)], copy_sem.at[h])
 
-    for h in range(strips):
-        load(h).start()
-    load_list = pltpu.make_async_copy(lists.at[0], list_s.at[z], list_load.at[0])
-    load_list.start()
 
     cx, cy = column // side, lax.rem(column, side)
     line_x = [(lax.rem(cx + hop, gx), y) for hop in range(1, gx)]
@@ -80,6 +76,10 @@
 
     for device in near:
         signal(barrier, device)
+    for h in range(strips):
+        load(h).start()
+    load_list = pltpu.make_async_copy(lists.at[0], list_s.at[z], list_load.at[0])
+    load_list.start()
     smalls = [
         pltpu.make_async_copy(source, target, small_sem.at[i])
         for i, (source, target) in enumerate(
@@ -376,8 +376,11 @@
         matrix = wide([q_left[h, tile] for tile in range(q_left.shape[1])])
         both = dot(matrix, wide([xh[0], xh[1]]))
         left = both[:n_size] + both[n_size:] + dot(matrix[:n_size], wide([xl[0], xl[1]]))
-        der[n, 0] -= left[:, n_size:]
-        der[n, 1] += left[:, :n_size]
+        re, im = der[n, 0] - left[:, n_size:], der[n, 1] + left[:, :n_size]
+        der[n, 0] = re
+        der[n, 1] = im
+        if h == strips - 1:
+            partial[...] += jnp.sum((re * re + im * im).reshape(n_size // 8, 8, n_size), axis=0)
 
     def finish_right(h, first, held):
         product = dot(wide([held[k] for k in range(modes)]), wide([q_right[0], q_right[1]]))
@@ -394,13 +397,17 @@
             finish_right(h, first, held[1])
             for n in range(2):
                 finish(h, first + n, *held[0][n])
-            for n in range(2):
-                build(h, jnp.minimum(first + 2, rows - 2) + n, n, coming)
-
-        @pl.loop(0, rows // 4)
+            if coming is not None:
+                for n in range(2):
+                    build(h, first + 2 + n, n, coming)
+
+        @pl.loop(0, rows // 4 - 1)
         def _(four):
             stage(four * 4, sets[0], sets[1])
             stage(four * 4 + 2, sets[1], sets[0])
+
+        stage(rows - 4, sets[0], sets[1])
+        stage(rows - 2, sets[1], None)
 
     def process(h):
         for level in range(length):
@@ -418,6 +425,7 @@
         if COMPUTE:
             compute(h)
 
+    partial[...] = jnp.zeros_like(partial)
     for h in range(strips):
         load_again(h).wait()
 
@@ -427,27 +435,29 @@
             process(h - 1)
     process(strips - 1)
 
-    def square(n, total):
-        re, im = der[n, 0], der[n, 1]
-        return total + jnp.sum((re * re + im * im).reshape(n_size // 8, 8, n_size), axis=0)
-
-    total = lax.fori_loop(0, rows, square, jnp.zeros((8, n_size), jnp.float32))
-    squares[...] = jnp.sum(total, axis=0, keepdims=True)
-
-    def copy_to(hop):
-        other = lax.rem(me + hop, count)
+    squares[...] = jnp.sum(partial[...], axis=0, keepdims=True)
+
+    def copy_to(hop, other):
         return pltpu.make_async_remote_copy(
             src_ref=squares,
             dst_ref=gathered.at[hop],
             send_sem=sum_send.at[0],
             recv_sem=sum_recv.at[0],
-            device_id=(other // gy, lax.rem(other, gy)),
+            device_id=other,
             device_id_type=MESH,
         )
 
-    @pl.loop(1, count)
-    def _(hop):
-        copy_to(hop).start()
+    for i in range(length):
+        level = jnp.where(2 * z < length, last - i, i)
+
+        @pl.loop(0, columns)
+        def _(step_on):
+            other = place(lax.rem(column + columns - 1 - step_on, columns), level)
+            hop = lax.rem(other[0] * gy + other[1] - me + count, count)
+
+            @pl.when(hop != 0)
+            def _():
+                copy_to(hop, other).start()
 
     out = pltpu.make_async_copy(der, negative, out_sem.at[0])
     out.start()
@@ -567,6 +577,7 @@
             vmem((1, n_size), f32),
             vmem((count, 1, n_size), f32),
             vmem((strips, few, parts, size, n_size) if direct else (1, 1, 1, 8, n_size), f32),
+            vmem((8, n_size), f32),
             dma((strips,)),
             dma((strips,)),
             dma((2,)),

time: 86.9 us -> 86.7 us (level)
  no operation moved by 1% of the time
where the time goes in v6:
time: 86.7 us; the launch traced here: 86.6 us
  Pallas kernels  83.6 us (96%)
  other arithmetic  1.62 us (2%)
  between operations  1.3 us (1%)
    pallas_call x1, Pallas kernels, body(): pl.pallas_call(functools.partial(kernel, gx, gy, length, strips, direct),...  83.6 us

profile of v6, /device:TPU:0, one launch (start us, length us, event | category | flops | bytes accessed | tf_op | source)
XLA Modules:
  0.0 86.6 jit_solution(7954855762617954247)
XLA Ops:
  1.3 0.0 copy-start
  1.3 83.6 %step.2 = (f32[8,2,128,128]{3,2,1,0:T(8,128)S(1)}, f32[1,128]{1,0:T(1,128)S(1)}) custom-call(s32[8,16]{1,0:T(8,128)} %up_ref.1, s32[8,16]{1,0:T(8,128)} %down_ref.1, s32[8,16]{1,0:T(8,128)} %occ_ref.1, f32[2,16]{1,0:T(2,128)} %coef_ref.1, f32[16]{0:T(128)} %rate_ref.1, f32[1]{0:T(128)S(6)} %copy.12.step, s32[1,1,32]{2,1,0:T(1,128)} %bitcast.4, ...), custom_call_target="tpu_custom_call" | custom-call | tf_op jit(solution)/shard_map/step/pallas_call | solution.py:603
  84.9 0.0 copy-done
  85.0 1.6 %multiply_subtract_fusion = (f32[8,2,128,128]{3,2,1,0:T(8,128)}, f32[8,2,128,128]{3,2,1,0:T(8,128)}) fusion(f32[8,2,128,128]{3,2,1,0:T(8,128)S(1)} %copy-done, f32[8,2,128,128]{3,2,1,0:T(8,128)S(1)} %get-tuple-element.4, f32[]{:T(128)S(1)} %bitcast.3), kind=kLoop, calls=%fused_computation | loop fusion | flops 786432 | bytes 4194308 | tf_op jit(solution)/shard_map/sub | solution.py:612
Async XLA Ops:
  1.3 83.7 %copy-start = (f32[8,2,128,128]{3,2,1,0:T(8,128)S(1)}, f32[8,2,128,128]{3,2,1,0:T(8,128)}, u32[]{:S(2)}) copy-start(f32[8,2,128,128]{3,2,1,0:T(8,128)} %state.1) | copy-start | bytes 3145732
